TPU v7x, 32 devices: a whole 2x2x4 slice. The times are simulated.
32 devices in a mesh: gx: 4 (over y, x), gy: 2 (over core), gz: 4 (over z).
Axes of the slice: x: 2, y: 2, z: 4, core: 2. Of those that a mesh axis runs over, the one named last changes fastest.
Arguments:
- rhs: float32 [8, 64, 64, 512], P(None, 'gx', 'gy', 'gz'), may hold values from -8 to 8
- stencil: float32 [14, 64, 64, 512], P(None, 'gx', 'gy', 'gz'), may hold values from 0.02 to 1
Outputs:
- solution: float32 [8, 64, 64, 512], P(None, 'gx', 'gy', 'gz')
- residual: float32 [8, 64, 64, 512], P(None, 'gx', 'gy', 'gz')
All inputs are finite; a program needn't handle non-finite values.
Results may differ from a plain program's by a relative error of at most 0.00029.
Values sent between devices are 32-bit elements; how exact they have to be, the bound alone decides.
A program may use at most 128 MiB of HBM per device.

v0:
```python
import jax
import jax.numpy as jnp
from jax import lax
from jax.sharding import PartitionSpec as P

ITERS = 2
FORWARD = [
    (a, b, c) for a in (-1, 0, 1) for b in (-1, 0, 1) for c in (-1, 0, 1) if (a, b, c) > (0, 0, 0)
]


def with_halo(cells, sides, width):
    for axis, dim in sides:
        count = lax.axis_size(axis)
        ends = count - 1
        head = lax.slice_in_dim(cells, 0, width, axis=dim)
        tail = lax.slice_in_dim(cells, cells.shape[dim] - width, cells.shape[dim], axis=dim)
        cells = jnp.concatenate(
            [
                lax.ppermute(tail, axis, [(i, (i + 1) % count) for i in range(ends)]),
                cells,
                lax.ppermute(head, axis, [((i + 1) % count, i) for i in range(ends)]),
            ],
            axis=dim,
        )
    return cells


def window(array, margin, depth, offset):
    result = array
    for place in range(3):
        dim = array.ndim - 3 + place
        inner = array.shape[dim] - 2 * margin
        begin = margin - depth + offset[place]
        result = lax.slice_in_dim(result, begin, begin + inner + 2 * depth, axis=dim)
    return result


def diagonal_field(padded, margin, depth):
    total = window(padded[0], margin, depth, (0, 0, 0))
    total = total + jnp.sum(window(padded[1:], margin, depth, (0, 0, 0)), axis=0)
    for index, offset in enumerate(FORWARD):
        back = (-offset[0], -offset[1], -offset[2])
        total = total + window(padded[index + 1], margin, depth, back)
    return total


def operate(field, fmargin, padded, smargin, diag, depth):
    result = diag[None] * window(field, fmargin, depth, (0, 0, 0))
    for index, offset in enumerate(FORWARD):
        back = (-offset[0], -offset[1], -offset[2])
        ahead_w = window(padded[index + 1], smargin, depth, (0, 0, 0))
        behind_w = window(padded[index + 1], smargin, depth, back)
        result = result - ahead_w[None] * window(field, fmargin, depth, offset)
        result = result - behind_w[None] * window(field, fmargin, depth, back)
    return result


def gram(left, right):
    flat_l = left.reshape(left.shape[0], -1)
    flat_r = right.reshape(right.shape[0], -1)
    return lax.dot_general(
        flat_l,
        flat_r,
        (((1,), (1,)), ((), ())),
        precision=lax.Precision.HIGHEST,
        preferred_element_type=jnp.float32,
    )


def combine(coef, field):
    return jnp.einsum("ij,ixyz->jxyz", coef, field, precision=lax.Precision.HIGHEST)


def small_dot(left, right):
    return jnp.dot(left, right, precision=lax.Precision.HIGHEST)


def solve_spd(matrix, right):
    factor = jnp.linalg.cholesky(matrix)
    return jax.scipy.linalg.cho_solve((factor, True), right)


def joint_sum(residual, direction, image):
    parts = (
        gram(residual, residual),
        gram(direction, image),
        gram(image, residual),
        gram(image, image),
    )
    return lax.psum((parts[0], parts[1], parts[2], parts[3]), ("gx", "gy", "gz"))


def shards(rhs, stencil):
    padded = with_halo(stencil, (("gx", 1), ("gy", 2), ("gz", 3)), 1)
    smargin = 1
    diag_full = diagonal_field(padded, 1, 0)
    direction = rhs
    dmargin = 0
    residual = direction
    rmargin = dmargin
    solution = jnp.zeros_like(rhs)
    norm_now = None
    for step in range(ITERS):
        field = with_halo(direction, (("gx", 1), ("gy", 2), ("gz", 3)), 1)
        fmargin = 1
        depth = 0
        image = operate(field, fmargin, padded, smargin, diag_full, depth)
        dir_here = window(field, fmargin, depth, (0, 0, 0))
        res_here = window(residual, rmargin, depth, (0, 0, 0))
        dir_core = window(dir_here, depth, 0, (0, 0, 0))
        res_core = window(res_here, depth, 0, (0, 0, 0))
        img_core = window(image, depth, 0, (0, 0, 0))
        norm_now, curve, cross, square = joint_sum(res_core, dir_core, img_core)
        alpha = solve_spd(curve, norm_now)
        solution = solution + combine(alpha, dir_core)
        res_here = res_here - combine(alpha, image)
        if step + 1 < ITERS:
            norm_next = (
                norm_now
                - small_dot(alpha.T, cross)
                - small_dot(cross.T, alpha)
                + small_dot(alpha.T, small_dot(square, alpha))
            )
            beta = solve_spd(norm_now, norm_next)
            direction = res_here + combine(beta, dir_here)
            norm_now = norm_next
        residual = res_here
        rmargin = depth
    return (solution, window(residual, rmargin, 0, (0, 0, 0)))


def solution(mesh):
    in_specs = (P(None, "gx", "gy", "gz"), P(None, "gx", "gy", "gz"))
    out_specs = (P(None, "gx", "gy", "gz"), P(None, "gx", "gy", "gz"))
    return jax.shard_map(shards, mesh=mesh, in_specs=in_specs, out_specs=out_specs, check_vma=False)
```

profile of v0, /device:TPU:0, one launch (start us, length us, event | category | flops | bytes accessed | tf_op | source)
XLA Modules:
  0.0 386.3 jit_solution(13203145947799155079)
XLA Ops:
  4.1 4.9 %collective-permute-start.6 = (f32[8,1,32,128]{3,0,2,1:T(8,128)S(1)}, f32[8,1,32,128]{3,0,2,1:T(8,128)S(1)}, u32[]{:S(2)}, u32[]{:S(2)}) collective-permute-start(f32[8,1,32,128]{3,0,2,1:T(8,128)S(1)} %get-tuple-element.64), channel_id=1, source_target_pairs={{0,8},{8,16},{16,24},{1,9},{9,17},{17,25},{2,10},{10,18},{18,26},{... | collective-permute-start | bytes 393224 | tf_op jit(solution)/shard_map/ppermute | solution.py:20
  18.4 9.2 %collective-permute-done.7 = f32[8,1,32,128]{3,0,2,1:T(8,128)S(1)} collective-permute-done((f32[8,1,32,128]{3,0,2,1:T(8,128)S(1)}, f32[8,1,32,128]{3,0,2,1:T(8,128)S(1)}, u32[]{:S(2)}, u32[]{:S(2)}) %collective-permute-start.7) | collective-permute-done | bytes 131104 | tf_op jit(solution)/shard_map/ppermute | solution.py:22
  42.3 4.5 %collective-permute-start.11 = (f32[8,18,34,1]{2,0,3,1:T(8,128)S(1)}, f32[8,18,34,1]{2,0,3,1:T(8,128)S(1)}, u32[]{:S(2)}, u32[]{:S(2)}) collective-permute-start(f32[8,18,34,1]{2,0,3,1:T(8,128)S(1)} %copy.176), channel_id=1, source_target_pairs={{0,1},{1,2},{2,3},{4,5},{5,6},{6,7},{8,9},{9,10},{10,11},{12,13},{... | collective-permute-start | bytes 58760 | tf_op jit(solution)/shard_map/ppermute | solution.py:20
  54.8 5.5 %convolution_bitcast_fusion.5 = f32[8,8]{0,1:T(8,128)} fusion(f32[8,16,32,128]{3,2,1,0:T(8,128)S(1)} %copy-done), kind=kOutput, calls=%fused_computation.145 | convolution fusion | flops 50331648 | bytes 2097408 | tf_op jit(solution)/shard_map/dot_general | solution.py:62
  68.6 5.6 %fusion.103 = (f32[14,18,34,1]{3,2,1,0:T(8,128)}, f32[14,18,34,1]{3,2,1,0:T(8,128)}) fusion(f32[14,18,34,128]{3,2,1,0:T(8,128)S(1)} %pad_maximum_fusion.1), kind=kLoop, calls=%fused_computation.230 | loop fusion | bytes 137088 | tf_op jit(solution)/shard_map/slice | solution.py:17
  74.2 3.9 %copy.164 = f32[14,18,34,1]{2,0,3,1:T(8,128)S(1)} copy(f32[14,18,34,1]{3,2,1,0:T(8,128)} %get-tuple-element.41) | data formatting | bytes 68544 | tf_op jit(solution)/shard_map/slice | solution.py:17
  81.7 3.9 %copy.165 = f32[14,18,34,1]{2,0,3,1:T(8,128)S(1)} copy(f32[14,18,34,1]{3,2,1,0:T(8,128)} %get-tuple-element.42) | data formatting | bytes 68544 | tf_op jit(solution)/shard_map/slice | solution.py:16
  87.2 8.0 %pad_maximum_fusion.2 = (f32[8,18,34,129]{3,0,2,1:T(8,128)}, f32[8,18,34,129]{3,0,2,1:T(8,128)}) fusion(f32[8,18,34,1]{3,0,2,1:T(8,128)} %copy.175, f32[8,18,1,128]{3,0,2,1:T(8,128)S(1)} %collective-permute-done.9, f32[8,18,32,128]{3,0,2,1:T(8,128)} %copy-done.4, f32[8,18,1,128]{3,0,2,1:T(8,128)S(1)} %collective-permute-done.8, f32[8,18,34,1]{3,0,2,1:T(8,128)} %copy.177), kind=kLoop, calls=%fused_computation.2 | loop fusion | flops 3789504 | bytes 7598592 | tf_op jit(solution)/shard_map/concatenate | solution.py:18
  102.2 13.3 %pad_maximum_fusion = f32[14,18,34,130]{3,2,1,0:T(8,128)} fusion(f32[14,18,34,1]{3,2,1,0:T(8,128)} %copy.167, f32[14,18,1,128]{3,2,1,0:T(1,128)S(1)} %copy.163, f32[14,18,32,128]{3,2,1,0:T(8,128)} %copy-done.5, f32[14,18,1,128]{3,2,1,0:T(1,128)S(1)} %copy.162, f32[14,18,34,1]{3,2,1,0:T(8,128)} %copy.166), kind=kLoop, calls=%fused_computation | loop fusion | flops 4455360 | bytes 8910720 | tf_op jit(solution)/shard_map/concatenate | solution.py:18
  115.5 8.0 %slice_bitcast_fusion.13 = (f32[16,34,130]{2,1,0:T(8,128)}, f32[1,16,34,130]{3,2,1,0:T(8,128)S(1)}, f32[1,16,34,130]{3,2,1,0:T(8,128)S(1)}, f32[1,16,34,130]{3,2...) fusion(f32[14,18,34,130]{3,2,1,0:T(8,128)} %pad_maximum_fusion), kind=kLoop, calls=%fused_computation.159 | loop fusion | bytes 10749440 | tf_op jit(solution)/shard_map/slice | solution.py:35
  146.1 31.7 %fusion.17 = f32[8,16,32,128]{3,0,2,1:T(8,128)} fusion(f32[8,18,32,128]{3,0,2,1:T(8,128)} %copy-done.4, f32[8,18,1,128]{3,0,2,1:T(8,128)S(1)} %collective-permute-done.8, f32[8,18,1,128]{3,0,2,1:T(8,128)S(1)} %collective-permute-done.9, f32[8,18,34,129]{3,0,2,1:T(8,128)} %get-tuple-element.52, f32[8,18,34,129]{3,0,2,1:T(8,128)} %get-tuple-element.51, ...), kind=kLoop, calls=%fused_computation.36 | loop fusion | flops 31981568 | bytes 51789824 | tf_op jit(solution)/shard_map/sub | solution.py:55
  177.8 6.7 %fusion.100 = f32[8,8,1,1]{1,0,3,2:T(8,128)S(1)} fusion(f32[8,16,32,128]{3,0,2,1:T(8,128)} %fusion.17, f32[8,16,32,128]{3,2,1,0:T(8,128)S(1)} %copy-done), kind=kOutput, calls=%fused_computation.227 | convolution fusion | flops 50331648 | bytes 4194560 | tf_op jit(solution)/shard_map/dot_general | solution.py:62
  184.6 4.7 %convolution_bitcast_fusion.4 = f32[8,8]{1,0:T(8,128)S(1)} fusion(f32[8,16,32,128]{3,0,2,1:T(8,128)S(1)} %copy-done.2), kind=kOutput, calls=%fused_computation.142 | convolution fusion | flops 50331648 | bytes 2097408 | tf_op jit(solution)/shard_map/dot_general | solution.py:62
  189.3 40.9 %all-reduce.1 = (f32[8,8]{0,1:T(8,128)S(1)}, f32[8,8]{0,1:T(8,128)S(1)}, f32[8,8]{1,0:T(8,128)S(1)}, f32[8,8]{1,0:T(8,128)S(1)}) all-reduce(f32[8,8]{0,1:T(8,128)S(1)} %copy-done.26, f32[8,8]{0,1:T(8,128)S(1)} %bitcast.147, f32[8,8]{1,0:T(8,128)S(1)} %bitcast.148, ...), channel_id=1, replica_groups=mesh['gx'=4,'gy'=2,'gz'=4] {'gx','gy','gz'}, use_global_device_ids=true, to_apply=%region_4.6 | all-reduce | flops 256 | bytes 2048 | tf_op jit(solution)/shard_map/psum | solution.py:91
  236.0 4.7 %convolution_subtract_fusion.1 = f32[8,16,32,128]{3,0,2,1:T(8,128)S(1)} fusion(f32[8,16,32,128]{3,0,2,1:T(8,128)} %fusion.17, f32[8,8]{1,0:T(8,128)S(1)} %fusion.90, f32[8,16,32,128]{3,2,1,0:T(8,128)S(1)} %copy-done), kind=kOutput, calls=%fused_computation.136 | convolution fusion | flops 50855936 | bytes 6291712 | tf_op jit(solution)/shard_map/ij,ixyz->jxyz/dot_general | solution.py:72
  244.8 4.2 %collective-permute-start.12 = (f32[8,1,32,128]{3,0,2,1:T(8,128)S(1)}, f32[8,1,32,128]{3,0,2,1:T(8,128)S(1)}, u32[]{:S(2)}, u32[]{:S(2)}) collective-permute-start(f32[8,1,32,128]{3,0,2,1:T(8,128)S(1)} %get-tuple-element.61), channel_id=1, source_target_pairs={{0,8},{8,16},{16,24},{1,9},{9,17},{17,25},{2,10},{10,18},{18,26},{... | collective-permute-start | bytes 393224 | tf_op jit(solution)/shard_map/ppermute | solution.py:20
  250.3 4.2 %fusion.95 = f32[8,16,32,128]{3,0,2,1:T(8,128)} fusion(f32[8,8]{1,0:T(8,128)S(1)} %fusion.90, f32[8,16,32,128]{3,2,1,0:T(8,128)S(1)} %copy-done.1), kind=kOutput, calls=%fused_computation.213 | convolution fusion | flops 50331648 | bytes 4194560 | tf_op jit(solution)/shard_map/ij,ixyz->jxyz/dot_general | solution.py:72
  258.7 5.3 %convolution_bitcast_fusion.1 = f32[8,8]{1,0:T(8,128)} fusion(f32[8,16,32,128]{3,0,2,1:T(8,128)S(1)} %convolution_subtract_fusion.1), kind=kOutput, calls=%fused_computation.138 | convolution fusion | flops 50331648 | bytes 2097408 | tf_op jit(solution)/shard_map/dot_general | solution.py:62
  275.5 5.2 %collective-permute-start.17 = (f32[8,18,34,1]{2,0,3,1:T(8,128)}, f32[8,18,34,1]{2,0,3,1:T(8,128)}, u32[]{:S(2)}, u32[]{:S(2)}) collective-permute-start(f32[8,18,34,1]{2,0,3,1:T(8,128)} %copy.217), channel_id=1, source_target_pairs={{0,1},{1,2},{2,3},{4,5},{5,6},{6,7},{8,9},{9,10},{10,11},{12,13},{... | collective-permute-start | bytes 58760 | tf_op jit(solution)/shard_map/ppermute | solution.py:20
  290.0 7.8 %pad_maximum_fusion.3 = (f32[8,18,34,129]{3,0,2,1:T(8,128)}, f32[8,18,34,129]{3,0,2,1:T(8,128)}) fusion(f32[8,18,34,1]{3,0,2,1:T(8,128)} %copy.216, f32[8,18,1,128]{3,0,2,1:T(8,128)S(1)} %collective-permute-done.15, f32[8,1,32,128]{3,0,2,1:T(8,128)S(1)} %collective-permute-done.13, f32[8,16,32,128]{3,0,2,1:T(8,128)S(1)} %convolution_add_fusion.1, ...), kind=kLoop, calls=%fused_computation.4 | loop fusion | flops 6315840 | bytes 7598592 | tf_op jit(solution)/shard_map/concatenate | solution.py:18
  297.8 29.8 %fusion.30 = f32[8,16,32,128]{3,0,2,1:T(8,128)} fusion(f32[8,18,34,129]{3,0,2,1:T(8,128)} %get-tuple-element.48, f32[8,18,34,129]{3,0,2,1:T(8,128)} %get-tuple-element.47, f32[8,18,33,128]{3,0,2,1:T(8,128)} %get-tuple-element.56, f32[8,18,33,128]{3,0,2,1:T(8,128)} %get-tuple-element.55, f32[8,16,32,128]{3,0,2,1:T(8,128)S(1)} %convolution_add_fusion.1, ...), kind=kLoop, calls=%fused_computation.50 | loop fusion | flops 28835840 | bytes 61865984 | tf_op jit(solution)/shard_map/sub | solution.py:55
  327.6 6.2 %convolution_bitcast_fusion.2 = f32[8,8]{0,1:T(8,128)S(1)} fusion(f32[8,16,32,128]{3,0,2,1:T(8,128)S(1)} %convolution_add_fusion.1, f32[8,16,32,128]{3,0,2,1:T(8,128)} %fusion.30), kind=kOutput, calls=%fused_computation.139 | convolution fusion | flops 50331648 | bytes 4194560 | tf_op jit(solution)/shard_map/dot_general | solution.py:62
  333.8 38.9 %all-reduce = (f32[8,8]{1,0:T(8,128)S(1)}, f32[8,8]{0,1:T(8,128)S(1)}) all-reduce(f32[8,8]{1,0:T(8,128)S(1)} %copy-done.25, f32[8,8]{0,1:T(8,128)S(1)} %convolution_bitcast_fusion.2), channel_id=1, replica_groups=mesh['gx'=4,'gy'=2,'gz'=4] {'gx','gy','gz'}, use_global_device_ids=true, to_apply=%region_8.11 | all-reduce | flops 128 | bytes 1024 | tf_op jit(solution)/shard_map/psum | solution.py:91
  375.9 4.1 %convolution_subtract_fusion = f32[8,16,32,128]{3,0,2,1:T(8,128)S(1)} fusion(f32[8,16,32,128]{3,0,2,1:T(8,128)} %copy-done.3, f32[8,8,1,1]{0,1,3,2:T(8,128)S(1)} %convolution_bitcast_fusion, f32[8,16,32,128]{3,0,2,1:T(8,128)} %fusion.30), kind=kOutput, calls=%fused_computation.133 | convolution fusion | flops 50855936 | bytes 6291712 | tf_op jit(solution)/shard_map/ij,ixyz->jxyz/dot_general | solution.py:72
  (189 shorter events, 123.2 us)
Async XLA Ops:
  0.6 16.1 %copy-start = (f32[8,16,32,128]{3,2,1,0:T(8,128)S(1)}, f32[8,16,32,128]{3,2,1,0:T(8,128)}, u32[]{:S(2)}) copy-start(f32[8,16,32,128]{3,2,1,0:T(8,128)} %param.5) | copy-start | bytes 6291460
  4.0 12.0 %copy-start.7 = (f32[8,16,32,128]{3,0,2,1:T(8,128)}, f32[8,16,32,128]{3,0,2,1:T(8,128)S(1)}, u32[]{:S(2)}) copy-start(f32[8,16,32,128]{3,0,2,1:T(8,128)S(1)} %copy.170) | copy-start | bytes 6291460
  4.1 12.0 %collective-permute-start.6 = (f32[8,1,32,128]{3,0,2,1:T(8,128)S(1)}, f32[8,1,32,128]{3,0,2,1:T(8,128)S(1)}, u32[]{:S(2)}, u32[]{:S(2)}) collective-permute-start(f32[8,1,32,128]{3,0,2,1:T(8,128)S(1)} %get-tuple-element.64), channel_id=1, source_target_pairs={{0,8},{8,16},{16,24},{1,9},{9,17},{17,25},{2,10},{10,18},{18,26},{... | collective-permute-start | bytes 393224 | tf_op jit(solution)/shard_map/ppermute | solution.py:20
  10.0 36.8 %collective-permute-start = (f32[14,1,32,128]{3,2,1,0:T(8,128)S(1)}, f32[14,1,32,128]{3,2,1,0:T(8,128)S(1)}, u32[]{:S(2)}, u32[]{:S(2)}) collective-permute-start(f32[14,1,32,128]{3,2,1,0:T(8,128)S(1)} %get-tuple-element.46), channel_id=1, source_target_pairs={{0,8},{8,16},{16,24},{1,9},{9,17},{17,25},{2,10},{10,18},{18,26},{... | collective-permute-start | bytes 688136 | tf_op jit(solution)/shard_map/ppermute | solution.py:20
  13.5 35.9 %collective-permute-start.1 = (f32[14,1,32,128]{3,2,1,0:T(8,128)S(1)}, f32[14,1,32,128]{3,2,1,0:T(8,128)S(1)}, u32[]{:S(2)}, u32[]{:S(2)}) collective-permute-start(f32[14,1,32,128]{3,2,1,0:T(8,128)S(1)} %get-tuple-element.45), channel_id=1, source_target_pairs={{8,0},{16,8},{24,16},{9,1},{17,9},{25,17},{10,2},{18,10},{26,18},{... | collective-permute-start | bytes 688136 | tf_op jit(solution)/shard_map/ppermute | solution.py:22
  14.8 12.9 %collective-permute-start.7 = (f32[8,1,32,128]{3,0,2,1:T(8,128)S(1)}, f32[8,1,32,128]{3,0,2,1:T(8,128)S(1)}, u32[]{:S(2)}, u32[]{:S(2)}) collective-permute-start(f32[8,1,32,128]{3,0,2,1:T(8,128)S(1)} %get-tuple-element.63), channel_id=1, source_target_pairs={{8,0},{16,8},{24,16},{9,1},{17,9},{25,17},{10,2},{18,10},{26,18},{... | collective-permute-start | bytes 393224 | tf_op jit(solution)/shard_map/ppermute | solution.py:22
  16.7 13.6 %copy-start.6 = (f32[14,16,32,128]{3,2,1,0:T(8,128)S(1)}, f32[14,16,32,128]{3,2,1,0:T(8,128)}, u32[]{:S(2)}) copy-start(f32[14,16,32,128]{3,2,1,0:T(8,128)} %param.6) | copy-start | bytes 11010052
  27.7 3.7 collective-permute-start.8
  29.0 3.2 collective-permute-start.9
  38.2 22.1 %collective-permute-start.10 = (f32[8,18,34,1]{2,0,3,1:T(8,128)S(1)}, f32[8,18,34,1]{2,0,3,1:T(8,128)S(1)}, u32[]{:S(2)}, u32[]{:S(2)}) collective-permute-start(f32[8,18,34,1]{2,0,3,1:T(8,128)S(1)} %copy.174), channel_id=1, source_target_pairs={{1,0},{2,1},{3,2},{5,4},{6,5},{7,6},{9,8},{10,9},{11,10},{13,12},{... | collective-permute-start | bytes 58760 | tf_op jit(solution)/shard_map/ppermute | solution.py:22
  42.3 20.7 %collective-permute-start.11 = (f32[8,18,34,1]{2,0,3,1:T(8,128)S(1)}, f32[8,18,34,1]{2,0,3,1:T(8,128)S(1)}, u32[]{:S(2)}, u32[]{:S(2)}) collective-permute-start(f32[8,18,34,1]{2,0,3,1:T(8,128)S(1)} %copy.176), channel_id=1, source_target_pairs={{0,1},{1,2},{2,3},{4,5},{5,6},{6,7},{8,9},{9,10},{10,11},{12,13},{... | collective-permute-start | bytes 58760 | tf_op jit(solution)/shard_map/ppermute | solution.py:20
  51.5 14.0 %collective-permute-start.2 = (f32[14,18,1,128]{3,0,2,1:T(8,128)S(1)}, f32[14,18,1,128]{3,0,2,1:T(8,128)S(1)}, u32[]{:S(2)}, u32[]{:S(2)}) collective-permute-start(f32[14,18,1,128]{3,0,2,1:T(8,128)S(1)} %copy.160), channel_id=1, source_target_pairs={{0,4},{1,5},{2,6},{3,7},{8,12},{9,13},{10,14},{11,15},{16,20},{17,... | collective-permute-start | bytes 387080 | tf_op jit(solution)/shard_map/ppermute | solution.py:20
  53.2 12.4 %collective-permute-start.3 = (f32[14,18,1,128]{3,0,2,1:T(8,128)S(1)}, f32[14,18,1,128]{3,0,2,1:T(8,128)S(1)}, u32[]{:S(2)}, u32[]{:S(2)}) collective-permute-start(f32[14,18,1,128]{3,0,2,1:T(8,128)S(1)} %copy.161), channel_id=1, source_target_pairs={{4,0},{5,1},{6,2},{7,3},{12,8},{13,9},{14,10},{15,11},{20,16},{21,... | collective-permute-start | bytes 387080 | tf_op jit(solution)/shard_map/ppermute | solution.py:22
  78.2 17.0 %collective-permute-start.4 = (f32[14,18,34,1]{2,0,3,1:T(8,128)S(1)}, f32[14,18,34,1]{2,0,3,1:T(8,128)S(1)}, u32[]{:S(2)}, u32[]{:S(2)}) collective-permute-start(f32[14,18,34,1]{2,0,3,1:T(8,128)S(1)} %copy.164), channel_id=1, source_target_pairs={{0,1},{1,2},{2,3},{4,5},{5,6},{6,7},{8,9},{9,10},{10,11},{12,13},{... | collective-permute-start | bytes 102824 | tf_op jit(solution)/shard_map/ppermute | solution.py:20
  85.6 13.1 %collective-permute-start.5 = (f32[14,18,34,1]{2,0,3,1:T(8,128)S(1)}, f32[14,18,34,1]{2,0,3,1:T(8,128)S(1)}, u32[]{:S(2)}, u32[]{:S(2)}) collective-permute-start(f32[14,18,34,1]{2,0,3,1:T(8,128)S(1)} %copy.165), channel_id=1, source_target_pairs={{1,0},{2,1},{3,2},{5,4},{6,5},{7,6},{9,8},{10,9},{11,10},{13,12},{... | collective-permute-start | bytes 102824 | tf_op jit(solution)/shard_map/ppermute | solution.py:22
  146.1 31.7 %copy-start.12 = (f32[16,32,128]{2,1,0:T(8,128)}, f32[16,32,128]{2,1,0:T(8,128)S(1)}, u32[]{:S(2)}) copy-start(f32[16,32,128]{2,1,0:T(8,128)S(1)} %get-tuple-element.69) | copy-start | bytes 786436
  177.8 6.7 %copy-start.2 = (f32[8,16,32,128]{3,0,2,1:T(8,128)S(1)}, f32[8,16,32,128]{3,0,2,1:T(8,128)}, u32[]{:S(2)}) copy-start(f32[8,16,32,128]{3,0,2,1:T(8,128)} %fusion.17) | copy-start | bytes 6291460
  240.7 18.0 %copy-start.3 = (f32[8,16,32,128]{3,0,2,1:T(8,128)}, f32[8,16,32,128]{3,0,2,1:T(8,128)S(1)}, u32[]{:S(2)}) copy-start(f32[8,16,32,128]{3,0,2,1:T(8,128)S(1)} %convolution_subtract_fusion.1) | copy-start | bytes 6291460
  244.8 9.7 %collective-permute-start.12 = (f32[8,1,32,128]{3,0,2,1:T(8,128)S(1)}, f32[8,1,32,128]{3,0,2,1:T(8,128)S(1)}, u32[]{:S(2)}, u32[]{:S(2)}) collective-permute-start(f32[8,1,32,128]{3,0,2,1:T(8,128)S(1)} %get-tuple-element.61), channel_id=1, source_target_pairs={{0,8},{8,16},{16,24},{1,9},{9,17},{17,25},{2,10},{10,18},{18,26},{... | collective-permute-start | bytes 393224 | tf_op jit(solution)/shard_map/ppermute | solution.py:20
  249.0 6.9 %collective-permute-start.13 = (f32[8,1,32,128]{3,0,2,1:T(8,128)S(1)}, f32[8,1,32,128]{3,0,2,1:T(8,128)S(1)}, u32[]{:S(2)}, u32[]{:S(2)}) collective-permute-start(f32[8,1,32,128]{3,0,2,1:T(8,128)S(1)} %get-tuple-element.62), channel_id=1, source_target_pairs={{8,0},{16,8},{24,16},{9,1},{17,9},{25,17},{10,2},{18,10},{26,18},{... | collective-permute-start | bytes 393224 | tf_op jit(solution)/shard_map/ppermute | solution.py:22
  255.9 8.1 %collective-permute-start.14 = (f32[8,18,1,128]{3,0,2,1:T(8,128)S(1)}, f32[8,18,1,128]{3,0,2,1:T(8,128)S(1)}, u32[]{:S(2)}, u32[]{:S(2)}) collective-permute-start(f32[8,18,1,128]{3,0,2,1:T(8,128)S(1)} %get-tuple-element.57), channel_id=1, source_target_pairs={{0,4},{1,5},{2,6},{3,7},{8,12},{9,13},{10,14},{11,15},{16,20},{17,... | collective-permute-start | bytes 221192 | tf_op jit(solution)/shard_map/ppermute | solution.py:20
  257.2 6.8 %collective-permute-start.15 = (f32[8,18,1,128]{3,0,2,1:T(8,128)S(1)}, f32[8,18,1,128]{3,0,2,1:T(8,128)S(1)}, u32[]{:S(2)}, u32[]{:S(2)}) collective-permute-start(f32[8,18,1,128]{3,0,2,1:T(8,128)S(1)} %get-tuple-element.58), channel_id=1, source_target_pairs={{4,0},{5,1},{6,2},{7,3},{12,8},{13,9},{14,10},{15,11},{20,16},{21,... | collective-permute-start | bytes 221192 | tf_op jit(solution)/shard_map/ppermute | solution.py:22
  270.7 12.4 %collective-permute-start.16 = (f32[8,18,34,1]{2,0,3,1:T(8,128)}, f32[8,18,34,1]{2,0,3,1:T(8,128)}, u32[]{:S(2)}, u32[]{:S(2)}) collective-permute-start(f32[8,18,34,1]{2,0,3,1:T(8,128)} %copy.215), channel_id=1, source_target_pairs={{1,0},{2,1},{3,2},{5,4},{6,5},{7,6},{9,8},{10,9},{11,10},{13,12},{... | collective-permute-start | bytes 58760 | tf_op jit(solution)/shard_map/ppermute | solution.py:22
  275.5 11.1 %collective-permute-start.17 = (f32[8,18,34,1]{2,0,3,1:T(8,128)}, f32[8,18,34,1]{2,0,3,1:T(8,128)}, u32[]{:S(2)}, u32[]{:S(2)}) collective-permute-start(f32[8,18,34,1]{2,0,3,1:T(8,128)} %copy.217), channel_id=1, source_target_pairs={{0,1},{1,2},{2,3},{4,5},{5,6},{6,7},{8,9},{9,10},{10,11},{12,13},{... | collective-permute-start | bytes 58760 | tf_op jit(solution)/shard_map/ppermute | solution.py:20
  (21 other events, 81.8 us)
where the time goes:
time: 393 us; the launch traced here: 386 us
  other arithmetic  107 us (27%)
  local copies, waits for them, and re-layouts  95.5 us (24%)
  blocking collectives  79.8 us (20%)
  matrix products  48.1 us (12%)
  starting transfers between devices  42.2 us (11%)
  waiting for transfers between devices  11.5 us (3%)
    psum x2, blocking collectives, joint_sum(): lax.psum((parts[0], parts[1], parts[2], parts[3]), ('gx', 'gy', 'gz'))  79.8 us
    sub x2, other arithmetic, operate(): result = result - behind_w[None] * window(field, fmargin, depth, back)  61.5 us
    concatenate x7, other arithmetic, with_halo(): jnp.concatenate([lax.ppermute(tail, axis, [(i, (i + 1) % count) for i in...  34.7 us
    ppermute x9, starting transfers between devices, with_halo(): lax.ppermute(tail, axis, [(i, (i + 1) % count) for i in range(ends)])  30 us
    dot_general x5, matrix products, gram(): lax.dot_general(flat_l, flat_r, (((1,), (1,)), ((), ())), precision=lax.P...  28.4 us
    slice x35, local copies, waits for them, and re-layouts, window(): lax.slice_in_dim(result, begin, begin + inner + 2 * depth, axis=dim)  28.3 us
    dot_general x5, matrix products, combine(): jnp.einsum('ij,ixyz->jxyz', coef, field, precision=lax.Precision.HIGHEST)  17.8 us
    slice x9, local copies, waits for them, and re-layouts, with_halo(): head = lax.slice_in_dim(cells, 0, width, axis=dim)  17.4 us
  transfers between devices with their start and end apart: 18, of which 3 were waited for; matrix products, arithmetic and copies ran while one was open for 16% of the time, Pallas kernels for 0%

commit v1 on v0

--- a/solution.py
+++ b/solution.py
@@ -7,6 +7,11 @@
 FORWARD = [
     (a, b, c) for a in (-1, 0, 1) for b in (-1, 0, 1) for c in (-1, 0, 1) if (a, b, c) > (0, 0, 0)
 ]
+
+
+def axis_by_axis(array_2, axis_one, axis_two):
+    half = lax.psum(array_2, axis_one)
+    return lax.psum(half, axis_two)
 
 
 def with_halo(cells, sides, width):
@@ -88,7 +93,7 @@
         gram(image, residual),
         gram(image, image),
     )
-    return lax.psum((parts[0], parts[1], parts[2], parts[3]), ("gx", "gy", "gz"))
+    return axis_by_axis((parts[0], parts[1], parts[2], parts[3]), ("gy", "gz"), "gx")
 
 
 def shards(rhs, stencil):

time: 393 us -> 380 us (0.967)
  blocking collectives: 79.8 us -> 68.7 us
    psum x2 -> x4, blocking collectives: 79.8 us -> 68.7 us  [the longest x2 43.8 us: axis_by_axis(): half = lax.psum(array_2, axis_one)]
where the time goes in v1:
time: 380 us; the launch traced here: 373 us
  other arithmetic  106 us (28%)
  local copies, waits for them, and re-layouts  95.7 us (25%)
  blocking collectives  68.7 us (18%)
  matrix products  48.1 us (13%)
  starting transfers between devices  41.3 us (11%)
  waiting for transfers between devices  11.6 us (3%)
    sub x2, other arithmetic, operate(): result = result - behind_w[None] * window(field, fmargin, depth, back)  60.2 us
    psum x2, blocking collectives, axis_by_axis(): half = lax.psum(array_2, axis_one)  43.8 us
    concatenate x7, other arithmetic, with_halo(): jnp.concatenate([lax.ppermute(tail, axis, [(i, (i + 1) % count) for i in...  34.6 us
    ppermute x9, starting transfers between devices, with_halo(): lax.ppermute(tail, axis, [(i, (i + 1) % count) for i in range(ends)])  28.5 us
    slice x35, local copies, waits for them, and re-layouts, window(): lax.slice_in_dim(result, begin, begin + inner + 2 * depth, axis=dim)  28.4 us
    dot_general x5, matrix products, gram(): lax.dot_general(flat_l, flat_r, (((1,), (1,)), ((), ())), precision=lax.P...  28.4 us
    psum x2, blocking collectives, axis_by_axis(): return lax.psum(half, axis_two)  24.9 us
    dot_general x5, matrix products, combine(): jnp.einsum('ij,ixyz->jxyz', coef, field, precision=lax.Precision.HIGHEST)  17.8 us
  transfers between devices with their start and end apart: 18, of which 3 were waited for; matrix products, arithmetic and copies ran while one was open for 16% of the time, Pallas kernels for 0%

profile of v1, /device:TPU:0, one launch (start us, length us, event | category | flops | bytes accessed | tf_op | source)
XLA Modules:
  0.0 372.9 jit_solution(9153637627434092762)
XLA Ops:
  4.1 4.9 %collective-permute-start.6 = (f32[8,1,32,128]{3,0,2,1:T(8,128)S(1)}, f32[8,1,32,128]{3,0,2,1:T(8,128)S(1)}, u32[]{:S(2)}, u32[]{:S(2)}) collective-permute-start(f32[8,1,32,128]{3,0,2,1:T(8,128)S(1)} %get-tuple-element.70), channel_id=1, source_target_pairs={{0,8},{8,16},{16,24},{1,9},{9,17},{17,25},{2,10},{10,18},{18,26},{... | collective-permute-start | bytes 393224 | tf_op jit(solution)/shard_map/ppermute | solution.py:25
  18.4 9.2 %collective-permute-done.7 = f32[8,1,32,128]{3,0,2,1:T(8,128)S(1)} collective-permute-done((f32[8,1,32,128]{3,0,2,1:T(8,128)S(1)}, f32[8,1,32,128]{3,0,2,1:T(8,128)S(1)}, u32[]{:S(2)}, u32[]{:S(2)}) %collective-permute-start.7) | collective-permute-done | bytes 131104 | tf_op jit(solution)/shard_map/ppermute | solution.py:27
  42.3 4.5 %collective-permute-start.11 = (f32[8,18,34,1]{2,0,3,1:T(8,128)S(1)}, f32[8,18,34,1]{2,0,3,1:T(8,128)S(1)}, u32[]{:S(2)}, u32[]{:S(2)}) collective-permute-start(f32[8,18,34,1]{2,0,3,1:T(8,128)S(1)} %copy.176), channel_id=1, source_target_pairs={{0,1},{1,2},{2,3},{4,5},{5,6},{6,7},{8,9},{9,10},{10,11},{12,13},{... | collective-permute-start | bytes 58760 | tf_op jit(solution)/shard_map/ppermute | solution.py:25
  54.9 5.5 %convolution_bitcast_fusion.5 = f32[8,8]{0,1:T(8,128)} fusion(f32[8,16,32,128]{3,2,1,0:T(8,128)S(1)} %copy-done), kind=kOutput, calls=%fused_computation.145 | convolution fusion | flops 50331648 | bytes 2097408 | tf_op jit(solution)/shard_map/dot_general | solution.py:67
  68.7 5.6 %fusion.103 = (f32[14,18,34,1]{3,2,1,0:T(8,128)}, f32[14,18,34,1]{3,2,1,0:T(8,128)}) fusion(f32[14,18,34,128]{3,2,1,0:T(8,128)S(1)} %pad_maximum_fusion.1), kind=kLoop, calls=%fused_computation.230 | loop fusion | bytes 137088 | tf_op jit(solution)/shard_map/slice | solution.py:22
  81.8 3.9 %copy.165 = f32[14,18,34,1]{2,0,3,1:T(8,128)S(1)} copy(f32[14,18,34,1]{3,2,1,0:T(8,128)} %get-tuple-element.48) | data formatting | bytes 68544 | tf_op jit(solution)/shard_map/slice | solution.py:21
  87.5 7.9 %pad_maximum_fusion.2 = (f32[8,18,34,129]{3,0,2,1:T(8,128)}, f32[8,18,34,129]{3,0,2,1:T(8,128)}) fusion(f32[8,18,34,1]{3,0,2,1:T(8,128)} %copy.175, f32[8,18,1,128]{3,0,2,1:T(8,128)S(1)} %collective-permute-done.9, f32[8,18,32,128]{3,0,2,1:T(8,128)} %copy-done.4, f32[8,18,1,128]{3,0,2,1:T(8,128)S(1)} %collective-permute-done.8, f32[8,18,34,1]{3,0,2,1:T(8,128)} %copy.177), kind=kLoop, calls=%fused_computation.2 | loop fusion | flops 3789504 | bytes 7598592 | tf_op jit(solution)/shard_map/concatenate | solution.py:23
  102.6 13.2 %pad_maximum_fusion = f32[14,18,34,130]{3,2,1,0:T(8,128)} fusion(f32[14,18,34,1]{3,2,1,0:T(8,128)} %copy.167, f32[14,18,1,128]{3,2,1,0:T(1,128)S(1)} %copy.163, f32[14,18,32,128]{3,2,1,0:T(8,128)} %copy-done.5, f32[14,18,1,128]{3,2,1,0:T(1,128)S(1)} %copy.162, f32[14,18,34,1]{3,2,1,0:T(8,128)} %copy.166), kind=kLoop, calls=%fused_computation | loop fusion | flops 4455360 | bytes 8910720 | tf_op jit(solution)/shard_map/concatenate | solution.py:23
  115.8 8.1 %slice_bitcast_fusion.13 = (f32[16,34,130]{2,1,0:T(8,128)}, f32[1,16,34,130]{3,2,1,0:T(8,128)S(1)}, f32[1,16,34,130]{3,2,1,0:T(8,128)S(1)}, f32[1,16,34,130]{3,2...) fusion(f32[14,18,34,130]{3,2,1,0:T(8,128)} %pad_maximum_fusion), kind=kLoop, calls=%fused_computation.159 | loop fusion | bytes 10749440 | tf_op jit(solution)/shard_map/slice | solution.py:40
  146.6 31.0 %fusion.17 = f32[8,16,32,128]{3,0,2,1:T(8,128)} fusion(f32[8,18,32,128]{3,0,2,1:T(8,128)} %copy-done.4, f32[8,18,1,128]{3,0,2,1:T(8,128)S(1)} %collective-permute-done.8, f32[8,18,1,128]{3,0,2,1:T(8,128)S(1)} %collective-permute-done.9, f32[8,18,34,129]{3,0,2,1:T(8,128)} %get-tuple-element.58, f32[8,18,34,129]{3,0,2,1:T(8,128)} %get-tuple-element.57, ...), kind=kLoop, calls=%fused_computation.36 | loop fusion | flops 31981568 | bytes 51789824 | tf_op jit(solution)/shard_map/sub | solution.py:60
  177.7 6.7 %fusion.100 = f32[8,8,1,1]{1,0,3,2:T(8,128)S(1)} fusion(f32[8,16,32,128]{3,0,2,1:T(8,128)} %fusion.17, f32[8,16,32,128]{3,2,1,0:T(8,128)S(1)} %copy-done), kind=kOutput, calls=%fused_computation.227 | convolution fusion | flops 50331648 | bytes 4194560 | tf_op jit(solution)/shard_map/dot_general | solution.py:67
  184.4 4.7 %convolution_bitcast_fusion.4 = f32[8,8]{1,0:T(8,128)S(1)} fusion(f32[8,16,32,128]{3,0,2,1:T(8,128)S(1)} %copy-done.2), kind=kOutput, calls=%fused_computation.142 | convolution fusion | flops 50331648 | bytes 2097408 | tf_op jit(solution)/shard_map/dot_general | solution.py:67
  189.1 29.5 %all-reduce.1 = (f32[8,8]{0,1:T(8,128)S(1)}, f32[8,8]{0,1:T(8,128)S(1)}, f32[8,8]{1,0:T(8,128)S(1)}, f32[8,8]{1,0:T(8,128)S(1)}) all-reduce(f32[8,8]{0,1:T(8,128)S(1)} %copy-done.26, f32[8,8]{0,1:T(8,128)S(1)} %bitcast.147, f32[8,8]{1,0:T(8,128)S(1)} %bitcast.148, ...), channel_id=1, replica_groups=mesh['gx'=4,'gy'=2,'gz'=4] {'gy','gz'}, use_global_device_ids=true, to_apply=%region_5.7 | all-reduce | flops 256 | bytes 2048 | tf_op jit(solution)/shard_map/psum | solution.py:13
  218.6 14.2 %all-reduce.3 = (f32[8,8]{0,1:T(8,128)S(1)}, f32[8,8]{0,1:T(8,128)S(1)}, f32[8,8]{1,0:T(8,128)S(1)}, f32[8,8]{1,0:T(8,128)S(1)}) all-reduce(f32[8,8]{0,1:T(8,128)S(1)} %get-tuple-element.14, f32[8,8]{0,1:T(8,128)S(1)} %get-tuple-element.15, f32[8,8]{1,0:T(8,128)S(1)} %get-tuple-element.16, ...), channel_id=1, replica_groups=mesh['gx'=4,'gy'=2,'gz'=4] {'gx'}, use_global_device_ids=true, to_apply=%region_6.8 | all-reduce | flops 256 | bytes 2048 | tf_op jit(solution)/shard_map/psum | solution.py:14
  238.6 4.7 %convolution_subtract_fusion.1 = f32[8,16,32,128]{3,0,2,1:T(8,128)S(1)} fusion(f32[8,16,32,128]{3,0,2,1:T(8,128)} %fusion.17, f32[8,8]{1,0:T(8,128)S(1)} %fusion.90, f32[8,16,32,128]{3,2,1,0:T(8,128)S(1)} %copy-done), kind=kOutput, calls=%fused_computation.136 | convolution fusion | flops 50855936 | bytes 6291712 | tf_op jit(solution)/shard_map/ij,ixyz->jxyz/dot_general | solution.py:77
  251.5 4.2 %fusion.95 = f32[8,16,32,128]{3,0,2,1:T(8,128)} fusion(f32[8,8]{1,0:T(8,128)S(1)} %fusion.90, f32[8,16,32,128]{3,2,1,0:T(8,128)S(1)} %copy-done.1), kind=kOutput, calls=%fused_computation.213 | convolution fusion | flops 50331648 | bytes 4194560 | tf_op jit(solution)/shard_map/ij,ixyz->jxyz/dot_general | solution.py:77
  260.2 5.3 %convolution_bitcast_fusion.1 = f32[8,8]{1,0:T(8,128)} fusion(f32[8,16,32,128]{3,0,2,1:T(8,128)S(1)} %convolution_subtract_fusion.1), kind=kOutput, calls=%fused_computation.138 | convolution fusion | flops 50331648 | bytes 2097408 | tf_op jit(solution)/shard_map/dot_general | solution.py:67
  276.9 5.2 %collective-permute-start.17 = (f32[8,18,34,1]{2,0,3,1:T(8,128)}, f32[8,18,34,1]{2,0,3,1:T(8,128)}, u32[]{:S(2)}, u32[]{:S(2)}) collective-permute-start(f32[8,18,34,1]{2,0,3,1:T(8,128)} %copy.217), channel_id=1, source_target_pairs={{0,1},{1,2},{2,3},{4,5},{5,6},{6,7},{8,9},{9,10},{10,11},{12,13},{... | collective-permute-start | bytes 58760 | tf_op jit(solution)/shard_map/ppermute | solution.py:25
  291.5 7.8 %pad_maximum_fusion.3 = (f32[8,18,34,129]{3,0,2,1:T(8,128)}, f32[8,18,34,129]{3,0,2,1:T(8,128)}) fusion(f32[8,18,34,1]{3,0,2,1:T(8,128)} %copy.216, f32[8,18,1,128]{3,0,2,1:T(8,128)S(1)} %collective-permute-done.15, f32[8,1,32,128]{3,0,2,1:T(8,128)S(1)} %collective-permute-done.13, f32[8,16,32,128]{3,0,2,1:T(8,128)S(1)} %convolution_add_fusion.1, ...), kind=kLoop, calls=%fused_computation.4 | loop fusion | flops 6315840 | bytes 7598592 | tf_op jit(solution)/shard_map/concatenate | solution.py:23
  299.3 29.1 %fusion.30 = f32[8,16,32,128]{3,0,2,1:T(8,128)} fusion(f32[8,18,34,129]{3,0,2,1:T(8,128)} %get-tuple-element.54, f32[8,18,34,129]{3,0,2,1:T(8,128)} %get-tuple-element.53, f32[8,18,33,128]{3,0,2,1:T(8,128)} %get-tuple-element.62, f32[8,18,33,128]{3,0,2,1:T(8,128)} %get-tuple-element.61, f32[8,16,32,128]{3,0,2,1:T(8,128)S(1)} %convolution_add_fusion.1, ...), kind=kLoop, calls=%fused_computation.50 | loop fusion | flops 28835840 | bytes 61865984 | tf_op jit(solution)/shard_map/sub | solution.py:60
  328.4 6.2 %convolution_bitcast_fusion.2 = f32[8,8]{0,1:T(8,128)S(1)} fusion(f32[8,16,32,128]{3,0,2,1:T(8,128)S(1)} %convolution_add_fusion.1, f32[8,16,32,128]{3,0,2,1:T(8,128)} %fusion.30), kind=kOutput, calls=%fused_computation.139 | convolution fusion | flops 50331648 | bytes 4194560 | tf_op jit(solution)/shard_map/dot_general | solution.py:67
  334.7 14.3 %all-reduce = (f32[8,8]{1,0:T(8,128)S(1)}, f32[8,8]{0,1:T(8,128)S(1)}) all-reduce(f32[8,8]{1,0:T(8,128)S(1)} %copy-done.25, f32[8,8]{0,1:T(8,128)S(1)} %convolution_bitcast_fusion.2), channel_id=1, replica_groups=mesh['gx'=4,'gy'=2,'gz'=4] {'gy','gz'}, use_global_device_ids=true, to_apply=%region_13.16 | all-reduce | flops 128 | bytes 1024 | tf_op jit(solution)/shard_map/psum | solution.py:13
  348.9 10.7 %all-reduce.2 = (f32[8,8]{1,0:T(8,128)S(1)}, f32[8,8]{0,1:T(8,128)S(1)}) all-reduce(f32[8,8]{1,0:T(8,128)S(1)} %get-tuple-element.12, f32[8,8]{0,1:T(8,128)S(1)} %get-tuple-element.13), channel_id=1, replica_groups=mesh['gx'=4,'gy'=2,'gz'=4] {'gx'}, use_global_device_ids=true, to_apply=%region_14.17 | all-reduce | flops 128 | bytes 1024 | tf_op jit(solution)/shard_map/psum | solution.py:14
  362.9 4.1 %convolution_subtract_fusion = f32[8,16,32,128]{3,0,2,1:T(8,128)S(1)} fusion(f32[8,16,32,128]{3,0,2,1:T(8,128)} %copy-done.3, f32[8,8,1,1]{0,1,3,2:T(8,128)S(1)} %convolution_bitcast_fusion, f32[8,16,32,128]{3,0,2,1:T(8,128)} %fusion.30), kind=kOutput, calls=%fused_computation.133 | convolution fusion | flops 50855936 | bytes 6291712 | tf_op jit(solution)/shard_map/ij,ixyz->jxyz/dot_general | solution.py:77
  (191 shorter events, 130.7 us)
Async XLA Ops:
  0.6 16.1 %copy-start = (f32[8,16,32,128]{3,2,1,0:T(8,128)S(1)}, f32[8,16,32,128]{3,2,1,0:T(8,128)}, u32[]{:S(2)}) copy-start(f32[8,16,32,128]{3,2,1,0:T(8,128)} %param.5) | copy-start | bytes 6291460
  4.0 12.0 %copy-start.7 = (f32[8,16,32,128]{3,0,2,1:T(8,128)}, f32[8,16,32,128]{3,0,2,1:T(8,128)S(1)}, u32[]{:S(2)}) copy-start(f32[8,16,32,128]{3,0,2,1:T(8,128)S(1)} %copy.170) | copy-start | bytes 6291460
  4.1 12.0 %collective-permute-start.6 = (f32[8,1,32,128]{3,0,2,1:T(8,128)S(1)}, f32[8,1,32,128]{3,0,2,1:T(8,128)S(1)}, u32[]{:S(2)}, u32[]{:S(2)}) collective-permute-start(f32[8,1,32,128]{3,0,2,1:T(8,128)S(1)} %get-tuple-element.70), channel_id=1, source_target_pairs={{0,8},{8,16},{16,24},{1,9},{9,17},{17,25},{2,10},{10,18},{18,26},{... | collective-permute-start | bytes 393224 | tf_op jit(solution)/shard_map/ppermute | solution.py:25
  10.0 36.8 %collective-permute-start = (f32[14,1,32,128]{3,2,1,0:T(8,128)S(1)}, f32[14,1,32,128]{3,2,1,0:T(8,128)S(1)}, u32[]{:S(2)}, u32[]{:S(2)}) collective-permute-start(f32[14,1,32,128]{3,2,1,0:T(8,128)S(1)} %get-tuple-element.52), channel_id=1, source_target_pairs={{0,8},{8,16},{16,24},{1,9},{9,17},{17,25},{2,10},{10,18},{18,26},{... | collective-permute-start | bytes 688136 | tf_op jit(solution)/shard_map/ppermute | solution.py:25
  13.5 35.9 %collective-permute-start.1 = (f32[14,1,32,128]{3,2,1,0:T(8,128)S(1)}, f32[14,1,32,128]{3,2,1,0:T(8,128)S(1)}, u32[]{:S(2)}, u32[]{:S(2)}) collective-permute-start(f32[14,1,32,128]{3,2,1,0:T(8,128)S(1)} %get-tuple-element.51), channel_id=1, source_target_pairs={{8,0},{16,8},{24,16},{9,1},{17,9},{25,17},{10,2},{18,10},{26,18},{... | collective-permute-start | bytes 688136 | tf_op jit(solution)/shard_map/ppermute | solution.py:27
  14.8 12.9 %collective-permute-start.7 = (f32[8,1,32,128]{3,0,2,1:T(8,128)S(1)}, f32[8,1,32,128]{3,0,2,1:T(8,128)S(1)}, u32[]{:S(2)}, u32[]{:S(2)}) collective-permute-start(f32[8,1,32,128]{3,0,2,1:T(8,128)S(1)} %get-tuple-element.69), channel_id=1, source_target_pairs={{8,0},{16,8},{24,16},{9,1},{17,9},{25,17},{10,2},{18,10},{26,18},{... | collective-permute-start | bytes 393224 | tf_op jit(solution)/shard_map/ppermute | solution.py:27
  16.7 13.6 %copy-start.6 = (f32[14,16,32,128]{3,2,1,0:T(8,128)S(1)}, f32[14,16,32,128]{3,2,1,0:T(8,128)}, u32[]{:S(2)}) copy-start(f32[14,16,32,128]{3,2,1,0:T(8,128)} %param.6) | copy-start | bytes 11010052
  27.7 3.7 collective-permute-start.8
  29.0 3.2 collective-permute-start.9
  38.2 22.2 %collective-permute-start.10 = (f32[8,18,34,1]{2,0,3,1:T(8,128)S(1)}, f32[8,18,34,1]{2,0,3,1:T(8,128)S(1)}, u32[]{:S(2)}, u32[]{:S(2)}) collective-permute-start(f32[8,18,34,1]{2,0,3,1:T(8,128)S(1)} %copy.174), channel_id=1, source_target_pairs={{1,0},{2,1},{3,2},{5,4},{6,5},{7,6},{9,8},{10,9},{11,10},{13,12},{... | collective-permute-start | bytes 58760 | tf_op jit(solution)/shard_map/ppermute | solution.py:27
  42.3 20.8 %collective-permute-start.11 = (f32[8,18,34,1]{2,0,3,1:T(8,128)S(1)}, f32[8,18,34,1]{2,0,3,1:T(8,128)S(1)}, u32[]{:S(2)}, u32[]{:S(2)}) collective-permute-start(f32[8,18,34,1]{2,0,3,1:T(8,128)S(1)} %copy.176), channel_id=1, source_target_pairs={{0,1},{1,2},{2,3},{4,5},{5,6},{6,7},{8,9},{9,10},{10,11},{12,13},{... | collective-permute-start | bytes 58760 | tf_op jit(solution)/shard_map/ppermute | solution.py:25
  51.5 14.1 %collective-permute-start.2 = (f32[14,18,1,128]{3,0,2,1:T(8,128)S(1)}, f32[14,18,1,128]{3,0,2,1:T(8,128)S(1)}, u32[]{:S(2)}, u32[]{:S(2)}) collective-permute-start(f32[14,18,1,128]{3,0,2,1:T(8,128)S(1)} %copy.160), channel_id=1, source_target_pairs={{0,4},{1,5},{2,6},{3,7},{8,12},{9,13},{10,14},{11,15},{16,20},{17,... | collective-permute-start | bytes 387080 | tf_op jit(solution)/shard_map/ppermute | solution.py:25
  53.3 12.5 %collective-permute-start.3 = (f32[14,18,1,128]{3,0,2,1:T(8,128)S(1)}, f32[14,18,1,128]{3,0,2,1:T(8,128)S(1)}, u32[]{:S(2)}, u32[]{:S(2)}) collective-permute-start(f32[14,18,1,128]{3,0,2,1:T(8,128)S(1)} %copy.161), channel_id=1, source_target_pairs={{4,0},{5,1},{6,2},{7,3},{12,8},{13,9},{14,10},{15,11},{20,16},{21,... | collective-permute-start | bytes 387080 | tf_op jit(solution)/shard_map/ppermute | solution.py:27
  78.3 17.2 %collective-permute-start.4 = (f32[14,18,34,1]{2,0,3,1:T(8,128)S(1)}, f32[14,18,34,1]{2,0,3,1:T(8,128)S(1)}, u32[]{:S(2)}, u32[]{:S(2)}) collective-permute-start(f32[14,18,34,1]{2,0,3,1:T(8,128)S(1)} %copy.164), channel_id=1, source_target_pairs={{0,1},{1,2},{2,3},{4,5},{5,6},{6,7},{8,9},{9,10},{10,11},{12,13},{... | collective-permute-start | bytes 102824 | tf_op jit(solution)/shard_map/ppermute | solution.py:25
  85.7 13.3 %collective-permute-start.5 = (f32[14,18,34,1]{2,0,3,1:T(8,128)S(1)}, f32[14,18,34,1]{2,0,3,1:T(8,128)S(1)}, u32[]{:S(2)}, u32[]{:S(2)}) collective-permute-start(f32[14,18,34,1]{2,0,3,1:T(8,128)S(1)} %copy.165), channel_id=1, source_target_pairs={{1,0},{2,1},{3,2},{5,4},{6,5},{7,6},{9,8},{10,9},{11,10},{13,12},{... | collective-permute-start | bytes 102824 | tf_op jit(solution)/shard_map/ppermute | solution.py:27
  146.6 31.1 %copy-start.12 = (f32[16,32,128]{2,1,0:T(8,128)}, f32[16,32,128]{2,1,0:T(8,128)S(1)}, u32[]{:S(2)}) copy-start(f32[16,32,128]{2,1,0:T(8,128)S(1)} %get-tuple-element.75) | copy-start | bytes 786436
  177.7 6.7 %copy-start.2 = (f32[8,16,32,128]{3,0,2,1:T(8,128)S(1)}, f32[8,16,32,128]{3,0,2,1:T(8,128)}, u32[]{:S(2)}) copy-start(f32[8,16,32,128]{3,0,2,1:T(8,128)} %fusion.17) | copy-start | bytes 6291460
  243.4 16.8 %copy-start.3 = (f32[8,16,32,128]{3,0,2,1:T(8,128)}, f32[8,16,32,128]{3,0,2,1:T(8,128)S(1)}, u32[]{:S(2)}) copy-start(f32[8,16,32,128]{3,0,2,1:T(8,128)S(1)} %convolution_subtract_fusion.1) | copy-start | bytes 6291460
  247.5 8.2 %collective-permute-start.12 = (f32[8,1,32,128]{3,0,2,1:T(8,128)S(1)}, f32[8,1,32,128]{3,0,2,1:T(8,128)S(1)}, u32[]{:S(2)}, u32[]{:S(2)}) collective-permute-start(f32[8,1,32,128]{3,0,2,1:T(8,128)S(1)} %get-tuple-element.67), channel_id=1, source_target_pairs={{0,8},{8,16},{16,24},{1,9},{9,17},{17,25},{2,10},{10,18},{18,26},{... | collective-permute-start | bytes 393224 | tf_op jit(solution)/shard_map/ppermute | solution.py:25
  250.2 7.0 %collective-permute-start.13 = (f32[8,1,32,128]{3,0,2,1:T(8,128)S(1)}, f32[8,1,32,128]{3,0,2,1:T(8,128)S(1)}, u32[]{:S(2)}, u32[]{:S(2)}) collective-permute-start(f32[8,1,32,128]{3,0,2,1:T(8,128)S(1)} %get-tuple-element.68), channel_id=1, source_target_pairs={{8,0},{16,8},{24,16},{9,1},{17,9},{25,17},{10,2},{18,10},{26,18},{... | collective-permute-start | bytes 393224 | tf_op jit(solution)/shard_map/ppermute | solution.py:27
  257.2 8.3 %collective-permute-start.14 = (f32[8,18,1,128]{3,0,2,1:T(8,128)S(1)}, f32[8,18,1,128]{3,0,2,1:T(8,128)S(1)}, u32[]{:S(2)}, u32[]{:S(2)}) collective-permute-start(f32[8,18,1,128]{3,0,2,1:T(8,128)S(1)} %get-tuple-element.63), channel_id=1, source_target_pairs={{0,4},{1,5},{2,6},{3,7},{8,12},{9,13},{10,14},{11,15},{16,20},{17,... | collective-permute-start | bytes 221192 | tf_op jit(solution)/shard_map/ppermute | solution.py:25
  258.5 7.0 %collective-permute-start.15 = (f32[8,18,1,128]{3,0,2,1:T(8,128)S(1)}, f32[8,18,1,128]{3,0,2,1:T(8,128)S(1)}, u32[]{:S(2)}, u32[]{:S(2)}) collective-permute-start(f32[8,18,1,128]{3,0,2,1:T(8,128)S(1)} %get-tuple-element.64), channel_id=1, source_target_pairs={{4,0},{5,1},{6,2},{7,3},{12,8},{13,9},{14,10},{15,11},{20,16},{21,... | collective-permute-start | bytes 221192 | tf_op jit(solution)/shard_map/ppermute | solution.py:27
  272.2 12.4 %collective-permute-start.16 = (f32[8,18,34,1]{2,0,3,1:T(8,128)}, f32[8,18,34,1]{2,0,3,1:T(8,128)}, u32[]{:S(2)}, u32[]{:S(2)}) collective-permute-start(f32[8,18,34,1]{2,0,3,1:T(8,128)} %copy.215), channel_id=1, source_target_pairs={{1,0},{2,1},{3,2},{5,4},{6,5},{7,6},{9,8},{10,9},{11,10},{13,12},{... | collective-permute-start | bytes 58760 | tf_op jit(solution)/shard_map/ppermute | solution.py:27
  276.9 11.1 %collective-permute-start.17 = (f32[8,18,34,1]{2,0,3,1:T(8,128)}, f32[8,18,34,1]{2,0,3,1:T(8,128)}, u32[]{:S(2)}, u32[]{:S(2)}) collective-permute-start(f32[8,18,34,1]{2,0,3,1:T(8,128)} %copy.217), channel_id=1, source_target_pairs={{0,1},{1,2},{2,3},{4,5},{5,6},{6,7},{8,9},{9,10},{10,11},{12,13},{... | collective-permute-start | bytes 58760 | tf_op jit(solution)/shard_map/ppermute | solution.py:25
  (21 other events, 81.9 us)
